TPU v7x, 32 devices: a whole 2x2x4 slice. The times are simulated.
32 devices in a mesh: row: 8 (over z, core), col: 4 (over y, x).
Axes of the slice: x: 2, y: 2, z: 4, core: 2. Of those that a mesh axis runs over, the one named last changes fastest.
Arguments:
- object_field: float32 [3, 2, 1024, 512], P(None, None, 'row', 'col'), may hold values from -5 to 5
- probe: float32 [2, 128, 128], replicated, may hold values from -5 to 5
- measured: float32 [8, 4, 2, 128, 128], P('row', 'col'), may hold values from 0.25 to 4
- positions: int32 [8, 4, 2, 2], P('row', 'col'), may hold values from 0 to 127
- counts: int32 [8, 4], P('row', 'col'), may hold values from 1 to 2, as said below
Outputs:
- object_next: float32 [3, 2, 1024, 512], P(None, None, 'row', 'col')
Inputs may be any that keep to these rules, and one draw needn't show every extreme that they name: Slots 0 to counts - 1 of a tile are live; some tile has all 2 live.
All inputs are finite; a program needn't handle non-finite values.
Results may differ from a plain program's by a relative error of at most 0.0003.
Values sent between devices are 32-bit elements; how exact they have to be, the bound alone decides.
A program may use at most 64 MiB of HBM per device.

v0:
```python
import functools

import jax
import jax.numpy as jnp
import ml_dtypes
import numpy as np
from jax import lax
from jax.experimental import pallas as pl
from jax.experimental.pallas import tpu as pltpu
from jax.sharding import PartitionSpec as P

ITERS = 2
LEARNING_RATE = 0.02


def halves_of(matrix):
    block = np.block([[matrix.real, matrix.imag], [-matrix.imag, matrix.real]])
    block = block.astype(np.float32)
    lead = block.astype(ml_dtypes.bfloat16)
    trail = (block - lead.astype(np.float32)).astype(ml_dtypes.bfloat16)
    return np.stack([lead, trail])


def make_tables(side):
    ordinal = np.arange(side)
    fourier = np.exp(-2j * np.pi / side * (np.outer(ordinal, ordinal) % side)) / np.sqrt(side)
    frequency = (ordinal + side // 2) % side - side // 2
    phase = np.exp(-0.25j * np.pi / side * frequency * frequency)
    spread = (fourier.conj() * phase[None, :]) @ fourier
    forms = [fourier, fourier.conj(), spread, spread.conj()]
    return np.stack([halves_of(form) for form in forms])


def split(values):
    lead = values.astype(jnp.bfloat16)
    return lead, (values - lead.astype(jnp.float32)).astype(jnp.bfloat16)


def dot(left, right):
    return jnp.dot(left, right, preferred_element_type=jnp.float32)


def both_sides(waves, table, form):
    side = waves[0][0].shape[0]
    stacked = jnp.concatenate([jnp.concatenate(pair, axis=1) for pair in waves], axis=0)
    lead, trail = split(stacked)
    right = (table[form, 0], table[form, 1])
    out = dot(lead, right[0]) + dot(trail, right[0]) + dot(lead, right[1])
    count = len(waves)
    turned = jnp.concatenate(
        [
            jnp.concatenate(
                [out[w * side : (w + 1) * side, part * side : (part + 1) * side] for w in range(count)],
                axis=1,
            )
            for part in range(2)
        ],
        axis=0,
    )
    lead, trail = split(turned)
    left = (table[form ^ 1, 0], table[form ^ 1, 1])
    out = dot(left[0], lead) + dot(left[0], trail) + dot(left[1], lead)
    return [
        tuple(
            out[part * side : (part + 1) * side, w * side : (w + 1) * side] for part in range(2)
        )
        for w in range(count)
    ]


def times(a, b):
    return (a[0] * b[0] - a[1] * b[1], a[0] * b[1] + a[1] * b[0])


def conj_times(a, b):
    return (a[0] * b[0] + a[1] * b[1], a[0] * b[1] - a[1] * b[0])


def masks_of(corners, window, side):
    half = side // 2
    found = []
    for dim in range(2):
        place = lax.broadcasted_iota(jnp.int32, (side, side), dim)
        corner = corners[0, 0, window, dim]
        found.append((place >= corner + half) | (place < corner - half))
    return found


def pack(tile):
    half = tile.shape[0] // 2
    lane = lax.broadcasted_iota(jnp.int32, (half, tile.shape[1]), 1)
    low, high = tile[:half], tile[half:]
    left = jnp.where(lane < half, low, pltpu.roll(high, half, 1))
    right = jnp.where(lane < half, pltpu.roll(low, half, 1), high)
    return left, right


def unpack(left, right):
    half = left.shape[0]
    lane = lax.broadcasted_iota(jnp.int32, left.shape, 1)
    low = jnp.where(lane < half, left, pltpu.roll(right, half, 1))
    high = jnp.where(lane < half, pltpu.roll(left, half, 1), right)
    return jnp.concatenate([low, high], axis=0)


PHASES = ("tall", "wide0", "wide1", "corner", "fold_rows", "fold_cols0", "fold_cols1")
RELAYED = ("wide1", "fold_cols1")


def step_kernel(
    shape, field, probe, samples, corners, count, table_far, out,
    table, later, vert, horz, diag, halo_out, halo_in, grad_rows, grad_in, grad_cols, fold_in,
    kept, relay, relay_send, relay_recv, pass_send, send_sem, recv_sem, table_sem,
):
    layer_count = field.shape[0]
    side = field.shape[-1]
    slots = samples.shape[0]
    half = side // 2
    windows = range(slots)
    slices = range(layer_count)
    me = {axis: lax.axis_index(axis) for axis in shape}
    has = {axis: (me[axis] > 0, me[axis] < shape[axis] - 1) for axis in shape}
    own = [field] + [later.at[t] for t in range(ITERS - 1)]
    parts = (pl.ds(0, half), pl.ds(half, half))
    detour = shape["col"] == 4

    def turns(phase, d):
        return (me["col"] == 2 - d) if detour and phase in RELAYED else None

    def both(here, phase, d):
        away = turns(phase, d)
        return here if away is None else jnp.logical_and(here, jnp.logical_not(away))

    def copy(phase, t, s, d, leg=0):
        if phase == "tall":
            axis, src, dst = "row", own[t].at[s, :, parts[d]], vert.at[t, s, :, parts[d]]
        elif phase.startswith("wide"):
            part = int(phase[-1])
            axis, src, dst = "col", halo_out.at[t, d, s, part], halo_in.at[t, d, s, part]
        elif phase == "corner":
            axis, src, dst = "row", horz.at[t, s, :, parts[d]], diag.at[t, s, :, parts[d]]
        elif phase == "fold_rows":
            rows = parts[1 - d]
            axis, src, dst = "row", grad_rows.at[t, s, :, :, rows], grad_in.at[t, s, :, :, rows]
        else:
            part = int(phase[-1])
            axis, src = "col", grad_cols.at[t, 1 - d, s, part]
            dst = fold_in.at[t, 1 - d, s, part]
        number = PHASES.index(phase)
        step = 1 if d else -1

        def moved(src, dst, sent, landed, step):
            return pltpu.make_async_remote_copy(
                src_ref=src,
                dst_ref=dst,
                send_sem=sent,
                recv_sem=landed,
                device_id={axis: me[axis] + step},
                device_id_type=pl.DeviceIdType.MESH,
            )

        landed = recv_sem.at[t, number, s, d]
        if leg == 0:
            return axis, dst, moved(src, dst, send_sem.at[t, number, s, d], landed, step)
        slot = (t, RELAYED.index(phase), s)
        if leg == 1:
            held = relay.at[slot]
            return axis, held, moved(src, held, relay_send.at[slot], relay_recv.at[slot], 2 * step)
        return axis, dst, moved(relay.at[slot], dst, pass_send.at[slot], landed, -step)

    def start(phase, t, s):
        for d in range(2):
            axis, _, moved = copy(phase, t, s, d)
            pl.when(both(has[axis][d], phase, d))(moved.start)
            if turns(phase, d) is not None:
                pl.when(turns(phase, d))(copy(phase, t, s, d, 1)[2].start)

    def hand_on(phase, t, s):
        for d in range(2):
            if turns(phase, d) is not None:

                @pl.when(me["col"] == (3 if d else 0))
                def forward():
                    copy(phase, t, s, d, 1)[2].wait_recv()
                    copy(phase, t, s, d, 2)[2].start()

    def arrive(phase, t, s):
        for d in range(2):
            axis, _, moved = copy(phase, t, s, d)
            pl.when(has[axis][1 - d])(moved.wait_recv)

    def uses():
        for t in range(ITERS):
            for phase in PHASES:
                for s in slices:
                    for d in range(2):
                        yield copy(phase, t, s, d) + (phase, d)

    load = pltpu.make_async_copy(table_far, table, table_sem)
    load.start()
    barrier = pltpu.get_barrier_semaphore()
    for axis in shape:
        for d in range(2):

            @pl.when(has[axis][d])
            def greet():
                pl.semaphore_signal(
                    barrier,
                    inc=1,
                    device_id={axis: me[axis] + (1 if d else -1)},
                    device_id_type=pl.DeviceIdType.MESH,
                )

    if detour:
        pl.semaphore_signal(
            barrier,
            inc=1,
            device_id={"col": lax.rem(me["col"] + 2, shape["col"])},
            device_id_type=pl.DeviceIdType.MESH,
        )

    def ship_wide(t, s):
        for part in range(2):
            for d, piece in enumerate(pack(own[t][s, part])):
                halo_out[t, d, s, part] = piece
        start("wide1", t, s)
        start("wide0", t, s)

    def ship_corner(t, s):
        arrive("wide0", t, s)
        arrive("wide1", t, s)
        for part in range(2):
            horz[t, s, part] = unpack(halo_in[t, 0, s, part], halo_in[t, 1, s, part])
        start("corner", t, s)

    peers = sum(there.astype(jnp.int32) for axis in shape for there in has[axis])
    pl.semaphore_wait(barrier, peers + (1 if detour else 0))
    for s in slices:
        start("tall", 0, s)
        ship_wide(0, s)
        if s > 0:
            hand_on("wide1", 0, s - 1)
    hand_on("wide1", 0, layer_count - 1)
    for axis, dst, _, _, d in uses():

        @pl.when(jnp.logical_not(has[axis][1 - d]))
        def clear():
            dst[...] = jnp.zeros(dst.shape, jnp.float32)

    masks = [masks_of(corners, w, side) for w in windows]
    beams = []
    for w in windows:
        shifts = [lax.rem(corners[0, 0, w, dim] + half, side) for dim in range(2)]
        beams.append(
            tuple(
                pltpu.roll(pltpu.roll(probe[part], shifts[0], 0), shifts[1], 1)
                for part in range(2)
            )
        )
    load.wait()

    def layer(t, s, w):
        rows, cols = masks[w]
        return tuple(
            jnp.where(
                rows,
                jnp.where(cols, diag[t, s, part], vert[t, s, part]),
                jnp.where(cols, horz[t, s, part], own[t][s, part]),
            )
            for part in range(2)
        )

    def gather_grads(t, s, pieces):
        for part in range(2):
            totals = [[0.0, 0.0], [0.0, 0.0]]
            for w in windows:
                rows, cols = masks[w]
                value = jnp.where(w < count[0, 0], pieces[w][part], 0.0)
                by_rows = (jnp.where(rows, 0.0, value), jnp.where(rows, value, 0.0))
                for a in range(2):
                    totals[a][0] += jnp.where(cols, 0.0, by_rows[a])
                    totals[a][1] += jnp.where(cols, by_rows[a], 0.0)
            for b in range(2):
                kept[b, s, part] = totals[0][b]
                grad_rows[t, s, b, part] = totals[1][b]
        start("fold_rows", t, s)

    def ship_cols(t, s):
        arrive("fold_rows", t, s)
        for part in range(2):
            aside = kept[1, s, part] + grad_in[t, s, 1, part]
            for d, piece in enumerate(pack(aside)):
                grad_cols[t, d, s, part] = piece
        start("fold_cols1", t, s)
        start("fold_cols0", t, s)

    def update(t, s, target):
        arrive("fold_cols0", t, s)
        arrive("fold_cols1", t, s)
        for part in range(2):
            inner = kept[0, s, part] + grad_in[t, s, 0, part]
            total = inner + unpack(fold_in[t, 0, s, part], fold_in[t, 1, s, part])
            target[s, part] = own[t][s, part] - LEARNING_RATE * total

    for t in range(ITERS):
        if t > 0:
            for s in slices:
                start("tall", t, s)
                ship_wide(t, s)
                if s > 0:
                    hand_on("wide1", t, s - 1)
            hand_on("wide1", t, layer_count - 1)
        waves = beams
        incident, layers = [], []
        ship_corner(t, 0)
        for s in slices:
            if s + 1 < layer_count:
                ship_corner(t, s + 1)
            arrive("tall", t, s)
            arrive("corner", t, s)
            incident.append(waves)
            layers.append([layer(t, s, w) for w in windows])
            waves = [times(layers[s][w], waves[w]) for w in windows]
            if s + 1 < layer_count:
                waves = both_sides(waves, table, 2)
        far = both_sides(waves, table, 0)
        scaled = []
        for w in windows:
            residue = far[w][0] * far[w][0] + far[w][1] * far[w][1] - samples[w]
            scaled.append((residue * far[w][0], residue * far[w][1]))
        back = both_sides(scaled, table, 1)
        for s in reversed(slices):
            gather_grads(t, s, [conj_times(incident[s][w], back[w]) for w in windows])
            if s + 1 < layer_count:
                ship_cols(t, s + 1)
            if s + 2 < layer_count:
                hand_on("fold_cols1", t, s + 2)
            if s > 0:
                back = both_sides(
                    [conj_times(layers[s][w], back[w]) for w in windows], table, 3
                )
        ship_cols(t, 0)
        for s in reversed(range(min(2, layer_count))):
            hand_on("fold_cols1", t, s)
        for s in reversed(slices):
            update(t, s, out if t + 1 == ITERS else own[t + 1])
    for axis, _, moved, phase, d in uses():
        pl.when(both(has[axis][d], phase, d))(moved.wait_send)
    for t in range(ITERS):
        for phase in RELAYED:
            for s in slices:
                for d in range(2):
                    if turns(phase, d) is not None:
                        pl.when(turns(phase, d))(copy(phase, t, s, d, 1)[2].wait_send)
                        pl.when(me["col"] == (3 if d else 0))(copy(phase, t, s, d, 2)[2].wait_send)


def shards(shape, object_field, probe, measured, positions, counts):
    samples = measured[0, 0]
    tables = make_tables(probe.shape[-1])
    vmem = pl.BlockSpec(memory_space=pltpu.VMEM)
    smem = pl.BlockSpec(memory_space=pltpu.SMEM)
    layer_count, _, side, _ = object_field.shape
    tiles = (layer_count, 2, side, side)
    packed = (ITERS, 2, layer_count, 2, side // 2, side)
    shapes = [
        (ITERS - 1,) + tiles,
        (ITERS,) + tiles,
        (ITERS,) + tiles,
        (ITERS,) + tiles,
        packed,
        packed,
        (ITERS, layer_count, 2, 2, side, side),
        (ITERS, layer_count, 2, 2, side, side),
        packed,
        packed,
        (2,) + tiles,
        (ITERS, len(RELAYED), layer_count, side // 2, side),
    ]
    relays = pltpu.SemaphoreType.DMA((ITERS, len(RELAYED), layer_count))
    sems = (ITERS, len(PHASES), layer_count, 2)
    return pl.pallas_call(
        functools.partial(step_kernel, shape),
        out_shape=jax.ShapeDtypeStruct(object_field.shape, jnp.float32),
        in_specs=[vmem, vmem, vmem, smem, smem, pl.BlockSpec(memory_space=pltpu.HBM)],
        out_specs=vmem,
        scratch_shapes=[pltpu.VMEM(tables.shape, jnp.bfloat16)]
        + [pltpu.VMEM(size, jnp.float32) for size in shapes]
        + [
            relays,
            relays,
            relays,
            pltpu.SemaphoreType.DMA(sems),
            pltpu.SemaphoreType.DMA(sems),
            pltpu.SemaphoreType.DMA,
        ],
        compiler_params=pltpu.CompilerParams(collective_id=0, has_side_effects=True),
        name="steps",
    )(object_field, probe, samples, positions, counts, jnp.asarray(tables))


def solution(mesh):
    placed = (
        P(None, None, "row", "col"),
        P(),
        P("row", "col", None, None, None),
        P("row", "col", None, None),
        P("row", "col"),
    )
    return jax.shard_map(
        functools.partial(shards, dict(mesh.shape)),
        mesh=mesh,
        in_specs=placed,
        out_specs=P(None, None, "row", "col"),
        check_vma=False,
    )
```

profile of v0, /device:TPU:18, one launch (start us, length us, event | category | flops | bytes accessed | tf_op | source)
XLA Modules:
  0.0 64.8 jit_solution(8809285570235446433)
XLA Ops:
  0.7 62.4 %steps.1 = f32[3,2,128,128]{3,2,1,0:T(8,128)} custom-call(f32[3,2,128,128]{3,2,1,0:T(8,128)} %field.1, f32[2,128,128]{2,1,0:T(8,128)} %probe.1, f32[2,128,128]{2,1,0:T(8,128)} %bitcast.1, s32[1,1,2,2]{3,2,1,0:T(2,128)} %corners.1, s32[1,1]{1,0:T(1,128)S(6)} %copy.8.count, bf16[4,2,256,256]{3,2,1,0:T(8,128)(2,1)} %constant.2.clone.table_far), custom_call_target="tpu_custom_call" | custom-call | tf_op jit(solution)/shard_map/steps/pallas_call | solution.py:382
  63.1 1.8 %copy.9 = f32[3,2,128,128]{3,2,1,0:T(8,128)} copy(f32[3,2,128,128]{3,2,1,0:T(8,128)} %steps.1) | data formatting | bytes 786432
where the time goes:
time: 65 us; the launch traced here: 64.8 us
  Pallas kernels  62.4 us (96%)
  local copies, waits for them, and re-layouts  1.77 us (3%)
  between operations  0.66 us (1%)
    pallas_call x1, Pallas kernels, shards(): pl.pallas_call(functools.partial(step_kernel, shape), out_shape=jax.Shape...  62.4 us
    unnamed x1, local copies, waits for them, and re-layouts  1.77 us

commit v1 on v0

v1 whole, which is shorter than its diff:
```python
import functools

import jax
import jax.numpy as jnp
import ml_dtypes
import numpy as np
from jax import lax
from jax.experimental import pallas as pl
from jax.experimental.pallas import tpu as pltpu
from jax.sharding import PartitionSpec as P

LEARNING_RATE = 0.02
COPIES = 192


def halves_of(matrix):
    block = np.block([[matrix.real, matrix.imag], [-matrix.imag, matrix.real]])
    block = block.astype(np.float32)
    lead = block.astype(ml_dtypes.bfloat16)
    trail = (block - lead.astype(np.float32)).astype(ml_dtypes.bfloat16)
    return np.stack([lead, trail])


def make_tables(side):
    ordinal = np.arange(side)
    fourier = np.exp(-2j * np.pi / side * (np.outer(ordinal, ordinal) % side)) / np.sqrt(side)
    frequency = (ordinal + side // 2) % side - side // 2
    phase = np.exp(-0.25j * np.pi / side * frequency * frequency)
    spread = (fourier.conj() * phase[None, :]) @ fourier
    forms = [fourier, fourier.conj(), spread, spread.conj()]
    return np.stack([halves_of(form) for form in forms])


def split(values):
    lead = values.astype(jnp.bfloat16)
    return lead, (values - lead.astype(jnp.float32)).astype(jnp.bfloat16)


def dot(left, right):
    return jnp.dot(left, right, preferred_element_type=jnp.float32)


def both_sides(waves, table, form):
    side = waves[0][0].shape[0]
    stacked = jnp.concatenate([jnp.concatenate(pair, axis=1) for pair in waves], axis=0)
    lead, trail = split(stacked)
    right = (table[form, 0], table[form, 1])
    out = dot(lead, right[0]) + dot(trail, right[0]) + dot(lead, right[1])
    count = len(waves)
    turned = jnp.concatenate(
        [
            jnp.concatenate(
                [out[w * side : (w + 1) * side, part * side : (part + 1) * side] for w in range(count)],
                axis=1,
            )
            for part in range(2)
        ],
        axis=0,
    )
    lead, trail = split(turned)
    left = (table[form ^ 1, 0], table[form ^ 1, 1])
    out = dot(left[0], lead) + dot(left[0], trail) + dot(left[1], lead)
    return [
        tuple(
            out[part * side : (part + 1) * side, w * side : (w + 1) * side] for part in range(2)
        )
        for w in range(count)
    ]


def times(a, b):
    return (a[0] * b[0] - a[1] * b[1], a[0] * b[1] + a[1] * b[0])


def conj_times(a, b):
    return (a[0] * b[0] + a[1] * b[1], a[0] * b[1] - a[1] * b[0])


def pack(tile):
    half = tile.shape[0] // 2
    lane = lax.broadcasted_iota(jnp.int32, (half, tile.shape[1]), 1)
    low, high = tile[:half], tile[half:]
    left = jnp.where(lane < half, low, pltpu.roll(high, half, 1))
    right = jnp.where(lane < half, pltpu.roll(low, half, 1), high)
    return left, right


def unpack(left, right):
    half = left.shape[0]
    lane = lax.broadcasted_iota(jnp.int32, left.shape, 1)
    low = jnp.where(lane < half, left, pltpu.roll(right, half, 1))
    high = jnp.where(lane < half, pltpu.roll(left, half, 1), right)
    return jnp.concatenate([low, high], axis=0)


def step_kernel(
    shape, field, probe, samples, corners, count, table_far, out,
    table, near, near_samples, near_corners, near_count, far_out, far_in, wide, tall,
    grads, grads_in, later, kept, grad_rows, grad_in, grad_cols, fold_in, relay,
    send_sem, recv_sem, table_sem,
):
    layer_count = field.shape[0]
    side = field.shape[-1]
    slots = samples.shape[0]
    half = side // 2
    slices = range(layer_count)
    row, col = lax.axis_index("row"), lax.axis_index("col")
    rows_all, cols_all = shape["row"], shape["col"]
    has_row = (row > 0, row < rows_all - 1)
    has_col = (col > 0, col < cols_all - 1)
    has_far = (col > 1, col < cols_all - 2)
    parts = (pl.ds(0, half), pl.ds(half, half))
    detour = cols_all == 4
    started = []
    numbers = {}

    def both(a, b):
        return jnp.logical_and(a, b)

    def passed_on(d):
        return (col == 2 - d) if detour else None

    def outer(d):
        return col == (3 if d else 0)

    def here(there, d):
        return both(there, jnp.logical_not(passed_on(d))) if detour else there

    def copy(key, src, dst, axis="col", step=0, passes=False):
        number = numbers.setdefault(key, len(numbers))
        sent = numbers.setdefault(key + ("passed",), len(numbers)) if passes else number
        return pltpu.make_async_remote_copy(
            src_ref=src,
            dst_ref=dst,
            send_sem=send_sem.at[sent],
            recv_sem=recv_sem.at[number],
            device_id={axis: (row if axis == "row" else col) + step},
            device_id_type=pl.DeviceIdType.MESH,
        )

    def start(when, moved):
        pl.when(when)(moved.start)
        started.append((when, moved))

    def arrive(when, moved):
        pl.when(when)(moved.wait_recv)

    def chunk(ref, k):
        return ref.at[0] if k == 0 else ref.at[1, parts[k - 1]]

    def near_copy(s, k, d, step=None, src=None):
        passes = src is not None
        src = src if passes else chunk(field.at[s], k)
        dst = chunk(near.at[1 - d, s], k)
        step = step if passes else 1 if d else -1
        return copy(("near", s, k, d), src, dst, "col", step, passes)

    def lend_copy(s, d):
        return copy(("lend", s), chunk(field.at[s], 2), relay.at[0, s], "col", 2 if d else -2)

    def samples_copy(d, step=None, src=None):
        passes = src is not None
        step = step if passes else 1 if d else -1
        src = src if passes else samples
        return copy(("samples", d), src, near_samples.at[1 - d], "col", step, passes)

    def corners_copy(d):
        return copy(("corners", d), corners.at[0, 0], near_corners.at[1 - d], "col", 1 if d else -1)

    def count_copy(d):
        return copy(("count", d), count, near_count.at[1 - d], "col", 1 if d else -1)

    def far_copy(s, d):
        return copy(("far", s, d), far_out.at[d, s], far_in.at[d, s], "col", 2 if d else -2)

    def tall_copy(i, s, d):
        ref = (field, near.at[0], near.at[1], wide)[i]
        src, dst = ref.at[s, :, parts[d]], tall.at[i, s, :, parts[d]]
        return copy(("tall", i, s, d), src, dst, "row", 1 if d else -1)

    def grads_copy(s, a, d):
        rows = parts[d ^ a]
        src, dst = grads.at[s, a, :, :, rows], grads_in.at[s, 1 - a, :, :, rows]
        return copy(("grads", s, a, d), src, dst, "row", 1 if d else -1)

    def fold_rows_copy(s, b, d):
        rows = parts[1 - d]
        src, dst = grad_rows.at[s, b, :, rows], grad_in.at[s, b, :, rows]
        return copy(("fold_rows", s, b, d), src, dst, "row", 1 if d else -1)

    def fold_cols_copy(s, part, d, leg=0):
        key = ("fold_cols", s, part, d)
        src, dst = grad_cols.at[1 - d, s, part], fold_in.at[1 - d, s, part]
        step = 1 if d else -1
        if leg == 0:
            return copy(key, src, dst, "col", step)
        held = relay.at[1, s]
        if leg == 1:
            return copy(("lend_cols", s), src, held, "col", 2 * step)
        return copy(key, held, dst, "col", -step)

    load = pltpu.make_async_copy(table_far, table, table_sem)
    load.start()
    barrier = pltpu.get_barrier_semaphore()
    meets = [("row", 1 if d else -1, has_row[d]) for d in range(2)]
    meets += [("col", 1 if d else -1, has_col[d]) for d in range(2)]
    meets += [("col", 2 if d else -2, has_far[d]) for d in range(2)]
    for axis, step, there in meets:

        @pl.when(there)
        def greet():
            pl.semaphore_signal(
                barrier,
                inc=1,
                device_id={axis: (row if axis == "row" else col) + step},
                device_id_type=pl.DeviceIdType.MESH,
            )

    pl.semaphore_wait(barrier, sum(there.astype(jnp.int32) for _, _, there in meets))

    def ship_near(s):
        for k in range(3):
            for d in range(2):
                start(here(has_col[d], d), near_copy(s, k, d))

    def ship_far(s):
        for part in range(2):
            for d, piece in enumerate(pack(field[s, part])):
                far_out[d, s, part] = piece
        for d in range(2):
            start(has_far[d], far_copy(s, d))
            if detour:
                start(passed_on(d), lend_copy(s, d))

    def hand_lent(s):
        if detour:
            for d in range(2):
                away = outer(d)
                arrive(away, lend_copy(s, d))
                start(away, near_copy(s, 2, d, -1 if d else 1, relay.at[0, s]))

    def hand_near(s):
        if detour:
            for k in range(2):
                for d in range(2):
                    away = outer(1 - d)
                    arrive(away, near_copy(s, k, 1 - d))
                    src = chunk(near.at[d, s], k)
                    start(away, near_copy(s, k, d, 2 if d else -2, src))

    def hand_samples():
        if detour:
            for d in range(2):
                away = outer(1 - d)
                arrive(away, samples_copy(1 - d))
                start(away, samples_copy(d, 2 if d else -2, near_samples.at[d]))

    def ship_samples(mine):
        for d in range(2):
            when = here(has_col[d], d)
            start(when if mine is None else both(when, mine), samples_copy(d))

    for d in range(2):
        start(has_col[d], corners_copy(d))
        start(has_col[d], count_copy(d))
    for s in slices:
        if s < 2:
            ship_near(s)
        for d in range(2):
            start(has_row[d], tall_copy(0, s, d))
        ship_far(s)

    def clear(when, *refs):
        @pl.when(jnp.logical_not(when))
        def fill():
            for ref in refs:
                ref[...] = jnp.zeros(ref.shape, ref.dtype)

    for d in range(2):
        clear(has_col[d], near.at[d], near_samples.at[d], tall.at[1 + d], fold_in.at[d])
        clear(has_far[1 - d], far_in.at[d])
        rows = parts[1 - d]
        for s in slices:
            clear(has_row[d], tall.at[0, s, :, rows], tall.at[3, s, :, rows])
            clear(has_row[d], tall.at[1, s, :, rows], tall.at[2, s, :, rows])
            clear(has_row[d], grads_in.at[s, 0, :, :, parts[d]], grads_in.at[s, 1, :, :, rows])
            clear(has_row[d], grad_in.at[s, :, :, parts[d]])

        @pl.when(jnp.logical_not(has_col[d]))
        def nobody():
            near_count[d, 0, 0] = 0
            for j in range(slots):
                for dim in range(2):
                    near_corners[d, j, dim] = 0

    lane = lax.broadcasted_iota(jnp.int32, (side, side), 1)
    first = lane < half

    class Window:
        pass

    def corner_of(k, j, dim):
        return corners[0, 0, j, dim] if k == 1 else near_corners[k // 2, j, dim]

    def window_of(k, j):
        found = Window()
        found.tile, found.slot = k, j
        masks = []
        for dim in range(2):
            place = lax.broadcasted_iota(jnp.int32, (side, side), dim)
            corner = corner_of(k, j, dim)
            masks.append((place >= corner + half) | (place < corner - half))
        found.rows, found.cols = masks
        shifts = [lax.rem(corner_of(k, j, dim) + half, side) for dim in range(2)]
        found.beam = tuple(
            pltpu.roll(pltpu.roll(probe[part], shifts[0], 0), shifts[1], 1) for part in range(2)
        )
        found.live = j < (count[0, 0] if k == 1 else near_count[k // 2, 0, 0])
        return found

    for d in range(2):
        arrive(has_col[1 - d], corners_copy(d))
        arrive(has_col[1 - d], count_copy(d))
    own_windows = [window_of(1, j) for j in range(slots)]
    side_windows = [window_of(k, j) for k in (0, 2) for j in range(slots)]
    load.wait()

    def relay_on(s):
        hand_lent(s)
        hand_near(s)

    def ship_tall(s):
        for d in range(2):
            for k in range(3):
                mine = has_col[1 - d]
                if detour and k < 2:
                    mine = both(mine, jnp.logical_not(outer(d)))
                arrive(mine, near_copy(s, k, d))
        for d in range(2):
            for e in range(2):
                start(both(has_row[d], has_col[e]), tall_copy(1 + e, s, d))
        for d in range(2):
            arrive(has_far[1 - d], far_copy(s, d))
        for part in range(2):
            wide[s, part] = unpack(far_in[0, s, part], far_in[1, s, part])
        for d in range(2):
            start(has_row[d], tall_copy(3, s, d))

    def land_tall(s):
        for i in range(4):
            for d in range(2):
                there = has_row[1 - d] if i in (0, 3) else both(has_row[1 - d], has_col[i - 1])
                arrive(there, tall_copy(i, s, d))

    def spread(tiles, beyond, k):
        if k == 1:
            return jnp.where(first, tiles[2], tiles[0])
        return jnp.where(first, tiles[1], beyond) if k == 0 else jnp.where(first, beyond, tiles[1])

    def cut(w, inner, across, down, slant):
        return tuple(
            jnp.where(
                w.rows,
                jnp.where(w.cols, slant[part], down[part]),
                jnp.where(w.cols, across[part], inner[part]),
            )
            for part in range(2)
        )

    def layers_first(s, windows):
        pieces = {}
        for k in range(3):
            tiles = [[near[0, s, p], field[s, p], near[1, s, p]] for p in range(2)]
            talls = [[tall[1, s, p], tall[0, s, p], tall[2, s, p]] for p in range(2)]
            pieces[k] = (
                [tiles[p][k] for p in range(2)],
                [spread(tiles[p], wide[s, p], k) for p in range(2)],
                [talls[p][k] for p in range(2)],
                [spread(talls[p], tall[3, s, p], k) for p in range(2)],
            )
        return [cut(w, *pieces[w.tile]) for w in windows]

    def residues(far, windows):
        scaled = []
        for w, value in zip(windows, far, strict=True):
            seen = samples[w.slot] if w.tile == 1 else near_samples[w.tile // 2, w.slot]
            residue = value[0] * value[0] + value[1] * value[1] - seen
            scaled.append((residue * value[0], residue * value[1]))
        return scaled

    def gather_first(s, windows, pieces):
        keep = jnp.zeros((side, side), jnp.float32)
        for part in range(2):
            totals = [[keep, keep], [keep, keep]]
            for w, piece in zip(windows, pieces, strict=True):
                value = jnp.where(w.live, piece[part], 0.0)
                inner, outside = jnp.where(w.cols, 0.0, value), jnp.where(w.cols, value, 0.0)
                if w.tile == 0:
                    inner, outside = jnp.where(first, outside, 0.0), jnp.where(first, 0.0, inner)
                elif w.tile == 2:
                    inner, outside = jnp.where(first, 0.0, outside), jnp.where(first, inner, 0.0)
                for b, share in enumerate((inner, outside)):
                    totals[0][b] += jnp.where(w.rows, 0.0, share)
                    totals[1][b] += jnp.where(w.rows, share, 0.0)
            for a in range(2):
                for b in range(2):
                    grads[s, a, b, part] = totals[a][b]

    def send_grads(s, a):
        for d in range(2):
            start(has_row[d], grads_copy(s, a, d))

    def renew(s):
        for a in range(2):
            for d in range(2):
                arrive(has_row[1 - d], grads_copy(s, a, d))
        top = lax.broadcasted_iota(jnp.int32, (side, side), 0) < half
        in_cols = jnp.where(first, has_col[1].astype(jnp.int32), has_col[0].astype(jnp.int32)) > 0
        in_rows = jnp.where(top, has_row[1].astype(jnp.int32), has_row[0].astype(jnp.int32)) > 0
        for part in range(2):
            tiles = [near[0, s, part], field[s, part], near[1, s, part]]
            talls = [tall[1, s, part], tall[0, s, part], tall[2, s, part]]
            before = [[tiles[1], spread(tiles, None, 1)], [talls[1], spread(talls, None, 1)]]
            for a in range(2):
                for b in range(2):
                    total = grads[s, a, b, part] + grads_in[s, a, b, part]
                    value = before[a][b] - LEARNING_RATE * total
                    if b:
                        value = jnp.where(in_cols, value, 0.0)
                    if a:
                        value = jnp.where(in_rows, value, 0.0)
                    later[a, b, s, part] = value

    def layers_second(s, windows):
        pieces = [[later[a, b, s, part] for part in range(2)] for a in range(2) for b in range(2)]
        return [cut(w, *pieces) for w in windows]

    windows = own_windows + side_windows
    waves = [w.beam for w in windows]
    incident, layers = [], []
    relay_on(0)
    for s in range(2, layer_count):
        ship_near(s)
    ends = jnp.logical_or(outer(0), outer(1))
    ship_samples(jnp.logical_not(ends) if detour else None)
    ship_tall(0)
    for s in range(1, layer_count):
        hand_lent(s)
    if detour:
        ship_samples(ends)
    for s in slices:
        if s + 1 < layer_count:
            hand_near(s + 1)
            ship_tall(s + 1)
        else:
            hand_samples()
        land_tall(s)
        incident.append(waves)
        layers.append(layers_first(s, windows))
        waves = [times(layer, wave) for layer, wave in zip(layers[s], waves, strict=True)]
        if s + 1 < layer_count:
            waves = both_sides(waves, table, 2)
    far = both_sides(waves, table, 0)
    for d in range(2):
        mine = has_col[1 - d]
        arrive(both(mine, jnp.logical_not(outer(d))) if detour else mine, samples_copy(d))
    back = both_sides(residues(far, windows), table, 1)
    for s in reversed(slices):
        pieces = [conj_times(a, b) for a, b in zip(incident[s], back, strict=True)]
        gather_first(s, windows, pieces)
        send_grads(s, 0)
        if s > 0:
            moved = [conj_times(a, b) for a, b in zip(layers[s], back, strict=True)]
            back = both_sides(moved, table, 3)
    for s in slices:
        send_grads(s, 1)

    windows = own_windows
    waves = [w.beam for w in windows]
    incident, layers = [], []
    for s in slices:
        renew(s)
        incident.append(waves)
        layers.append(layers_second(s, windows))
        waves = [times(layer, wave) for layer, wave in zip(layers[s], waves, strict=True)]
        if s + 1 < layer_count:
            waves = both_sides(waves, table, 2)
    far = both_sides(waves, table, 0)
    back = both_sides(residues(far, windows), table, 1)

    def gather_second(s, pieces):
        for part in range(2):
            totals = [[0.0, 0.0], [0.0, 0.0]]
            for w, piece in zip(windows, pieces, strict=True):
                value = jnp.where(w.live, piece[part], 0.0)
                by_rows = (jnp.where(w.rows, 0.0, value), jnp.where(w.rows, value, 0.0))
                for a in range(2):
                    totals[a][0] += jnp.where(w.cols, 0.0, by_rows[a])
                    totals[a][1] += jnp.where(w.cols, by_rows[a], 0.0)
            for b in range(2):
                kept[b, s, part] = totals[0][b]
                grad_rows[s, b, part] = totals[1][b]
        for d in range(2):
            start(has_row[d], fold_rows_copy(s, 1, d))

    def ship_cols(s):
        for d in range(2):
            arrive(has_row[1 - d], fold_rows_copy(s, 1, d))
        for part in range(2):
            aside = kept[1, s, part] + grad_in[s, 1, part]
            for d, piece in enumerate(pack(aside)):
                grad_cols[d, s, part] = piece
        for part in (1, 0):
            for d in range(2):
                when = here(has_col[d], d) if part else has_col[d]
                start(when, fold_cols_copy(s, part, d))
                if detour and part:
                    start(passed_on(d), fold_cols_copy(s, part, d, 1))

    def hand_cols(s):
        if detour:
            for d in range(2):
                arrive(outer(d), fold_cols_copy(s, 1, d, 1))
                start(outer(d), fold_cols_copy(s, 1, d, 2))

    def finish(s):
        for d in range(2):
            arrive(has_row[1 - d], fold_rows_copy(s, 0, d))
            for part in range(2):
                arrive(has_col[1 - d], fold_cols_copy(s, part, d))
        for part in range(2):
            inner = kept[0, s, part] + grad_in[s, 0, part]
            total = inner + unpack(fold_in[0, s, part], fold_in[1, s, part])
            out[s, part] = later[0, 0, s, part] - LEARNING_RATE * total

    for s in reversed(slices):
        gather_second(s, [conj_times(a, b) for a, b in zip(incident[s], back, strict=True)])
        if s + 1 < layer_count:
            ship_cols(s + 1)
        if s > 0:
            moved = [conj_times(a, b) for a, b in zip(layers[s], back, strict=True)]
            back = both_sides(moved, table, 3)
    for s in reversed(slices):
        for d in range(2):
            start(has_row[d], fold_rows_copy(s, 0, d))
    for s in range(layer_count - 1, 1, -1):
        hand_cols(s)
    ship_cols(0)
    for s in reversed(range(min(2, layer_count))):
        hand_cols(s)
    for s in reversed(slices):
        finish(s)
    for when, moved in started:
        pl.when(when)(moved.wait_send)
    assert len(numbers) <= COPIES


def shards(shape, object_field, probe, measured, positions, counts):
    samples = measured[0, 0]
    tables = make_tables(probe.shape[-1])
    vmem = pl.BlockSpec(memory_space=pltpu.VMEM)
    smem = pl.BlockSpec(memory_space=pltpu.SMEM)
    layer_count, _, side, _ = object_field.shape
    tiles = (layer_count, 2, side, side)
    packed = (2, layer_count, 2, side // 2, side)
    pair = (layer_count, 2, 2, 2, side, side)
    f32 = [
        pltpu.VMEM(size, jnp.float32)
        for size in (
            packed,
            packed,
            tiles,
            (4,) + tiles,
            pair,
            pair,
            (2, 2) + tiles,
            (2,) + tiles,
            (layer_count, 2, 2, side, side),
            (layer_count, 2, 2, side, side),
            packed,
            packed,
            (2, layer_count, side // 2, side),
        )
    ]
    return pl.pallas_call(
        functools.partial(step_kernel, shape),
        out_shape=jax.ShapeDtypeStruct(object_field.shape, jnp.float32),
        in_specs=[vmem, vmem, vmem, smem, smem, pl.BlockSpec(memory_space=pltpu.HBM)],
        out_specs=vmem,
        scratch_shapes=[
            pltpu.VMEM(tables.shape, jnp.bfloat16),
            pltpu.VMEM((2,) + tiles, jnp.float32),
            pltpu.VMEM((2,) + samples.shape, jnp.float32),
            pltpu.SMEM((2,) + positions.shape[2:], jnp.int32),
            pltpu.SMEM((2,) + counts.shape, jnp.int32),
        ]
        + f32
        + [
            pltpu.SemaphoreType.DMA((COPIES,)),
            pltpu.SemaphoreType.DMA((COPIES,)),
            pltpu.SemaphoreType.DMA,
        ],
        compiler_params=pltpu.CompilerParams(collective_id=0, has_side_effects=True),
        name="steps",
    )(object_field, probe, samples, positions, counts, jnp.asarray(tables))


def solution(mesh):
    placed = (
        P(None, None, "row", "col"),
        P(),
        P("row", "col", None, None, None),
        P("row", "col", None, None),
        P("row", "col"),
    )
    return jax.shard_map(
        functools.partial(shards, dict(mesh.shape)),
        mesh=mesh,
        in_specs=placed,
        out_specs=P(None, None, "row", "col"),
        check_vma=False,
    )
```

time: 65 us -> 56.9 us (0.88)
  Pallas kernels: 62.4 us -> 54.1 us
    pallas_call x1, Pallas kernels: 62.4 us -> 54.1 us  [shards(): pl.pallas_call(functools.partial(step_kernel, shape), out_shape=jax.Shape...]
where the time goes in v1:
time: 56.9 us; the launch traced here: 56.5 us
  Pallas kernels  54.1 us (95%)
  local copies, waits for them, and re-layouts  1.77 us (3%)
  between operations  0.66 us (1%)
    pallas_call x1, Pallas kernels, shards(): pl.pallas_call(functools.partial(step_kernel, shape), out_shape=jax.Shape...  54.1 us
    unnamed x1, local copies, waits for them, and re-layouts  1.77 us

profile of v1, /device:TPU:18, one launch (start us, length us, event | category | flops | bytes accessed | tf_op | source)
XLA Modules:
  0.0 56.5 jit_solution(6805633572163796759)
XLA Ops:
  0.7 54.1 %steps.1 = f32[3,2,128,128]{3,2,1,0:T(8,128)} custom-call(f32[3,2,128,128]{3,2,1,0:T(8,128)} %field.1, f32[2,128,128]{2,1,0:T(8,128)} %probe.1, f32[2,128,128]{2,1,0:T(8,128)} %bitcast.1, s32[1,1,2,2]{3,2,1,0:T(2,128)} %corners.1, s32[1,1]{1,0:T(1,128)S(6)} %copy.8.count, bf16[4,2,256,256]{3,2,1,0:T(8,128)(2,1)} %constant.2.clone.table_far), custom_call_target="tpu_custom_call" | custom-call | tf_op jit(solution)/shard_map/steps/pallas_call | solution.py:585
  54.8 1.8 %copy.9 = f32[3,2,128,128]{3,2,1,0:T(8,128)} copy(f32[3,2,128,128]{3,2,1,0:T(8,128)} %steps.1) | data formatting | bytes 786432

commit v2 on v1

--- a/solution.py
+++ b/solution.py
@@ -94,10 +94,10 @@
 
 
 def step_kernel(
-    shape, field, probe, samples, corners, count, table_far, out,
-    table, near, near_samples, near_corners, near_count, far_out, far_in, wide, tall,
+    shape, field_far, probe_far, samples_far, corners, count, table_far, out,
+    field, probe, samples, table, near, near_samples, near_corners, near_count, far_out, far_in, wide, tall,
     grads, grads_in, later, kept, grad_rows, grad_in, grad_cols, fold_in, relay,
-    send_sem, recv_sem, table_sem,
+    send_sem, recv_sem, load_sem,
 ):
     layer_count = field.shape[0]
     side = field.shape[-1]
@@ -108,6 +108,14 @@
     rows_all, cols_all = shape["row"], shape["col"]
     has_row = (row > 0, row < rows_all - 1)
     has_col = (col > 0, col < cols_all - 1)
+    loads = [
+        pltpu.make_async_copy(src, dst, load_sem.at[i])
+        for i, (src, dst) in enumerate(
+            ((field_far, field), (probe_far, probe), (table_far, table), (samples_far, samples))
+        )
+    ]
+    for load in loads:
+        load.start()
     has_far = (col > 1, col < cols_all - 2)
     parts = (pl.ds(0, half), pl.ds(half, half))
     detour = cols_all == 4
@@ -164,19 +172,23 @@
         src = src if passes else samples
         return copy(("samples", d), src, near_samples.at[1 - d], "col", step, passes)
 
-    def corners_copy(d):
-        return copy(("corners", d), corners.at[0, 0], near_corners.at[1 - d], "col", 1 if d else -1)
-
-    def count_copy(d):
-        return copy(("count", d), count, near_count.at[1 - d], "col", 1 if d else -1)
+    def place_copies(d, step=None):
+        passes = step is not None
+        step = step if passes else 1 if d else -1
+        src = (near_corners.at[d], near_count.at[d]) if passes else (corners.at[0, 0], count)
+        dst = (near_corners.at[1 - d], near_count.at[1 - d])
+        return [
+            copy(("place", i, d), *pair, "col", step, passes)
+            for i, pair in enumerate(zip(src, dst, strict=True))
+        ]
 
     def far_copy(s, d):
         return copy(("far", s, d), far_out.at[d, s], far_in.at[d, s], "col", 2 if d else -2)
 
-    def tall_copy(i, s, d):
+    def tall_copy(i, s, part, d):
         ref = (field, near.at[0], near.at[1], wide)[i]
-        src, dst = ref.at[s, :, parts[d]], tall.at[i, s, :, parts[d]]
-        return copy(("tall", i, s, d), src, dst, "row", 1 if d else -1)
+        src, dst = ref.at[s, part, parts[d]], tall.at[i, s, part, parts[d]]
+        return copy(("tall", i, s, part, d), src, dst, "row", 1 if d else -1)
 
     def grads_copy(s, a, d):
         rows = parts[d ^ a]
@@ -199,11 +211,9 @@
             return copy(("lend_cols", s), src, held, "col", 2 * step)
         return copy(key, held, dst, "col", -step)
 
-    load = pltpu.make_async_copy(table_far, table, table_sem)
-    load.start()
     barrier = pltpu.get_barrier_semaphore()
     meets = [("row", 1 if d else -1, has_row[d]) for d in range(2)]
-    meets += [("col", 1 if d else -1, has_col[d]) for d in range(2)]
+    meets += [("col", 1 if d else -1, here(has_col[d], d)) for d in range(2)]
     meets += [("col", 2 if d else -2, has_far[d]) for d in range(2)]
     for axis, step, there in meets:
 
@@ -216,17 +226,12 @@
                 device_id_type=pl.DeviceIdType.MESH,
             )
 
-    pl.semaphore_wait(barrier, sum(there.astype(jnp.int32) for _, _, there in meets))
-
     def ship_near(s):
         for k in range(3):
             for d in range(2):
                 start(here(has_col[d], d), near_copy(s, k, d))
 
     def ship_far(s):
-        for part in range(2):
-            for d, piece in enumerate(pack(field[s, part])):
-                far_out[d, s, part] = piece
         for d in range(2):
             start(has_far[d], far_copy(s, d))
             if detour:
@@ -239,14 +244,60 @@
                 arrive(away, lend_copy(s, d))
                 start(away, near_copy(s, 2, d, -1 if d else 1, relay.at[0, s]))
 
-    def hand_near(s):
+    def relayed_to(d):
+        return (col == 1 + d) if detour else None
+
+    def ship_tall(when, i, s, part, d):
+        start(both(when, has_row[d]), tall_copy(i, s, part, d))
+
+    def ship_piece(when, i, s, k):
+        if k == 0:
+            for d in range(2):
+                ship_tall(when, i, s, 0, d)
+        else:
+            ship_tall(when, i, s, 1, k - 1)
+
+    def take_direct(s):
+        for k in range(3):
+            for d in range(2):
+                mine = has_col[1 - d]
+                if detour:
+                    mine = both(mine, jnp.logical_not(relayed_to(d)))
+                arrive(mine, near_copy(s, k, d))
+                if detour and k < 2:
+                    src = chunk(near.at[1 - d, s], k)
+                    start(outer(d), near_copy(s, k, 1 - d, -2 if d else 2, src))
+                ship_piece(mine, 2 - d, s, k)
+
+    def take_relayed(s):
         if detour:
-            for k in range(2):
+            for k in range(3):
                 for d in range(2):
-                    away = outer(1 - d)
-                    arrive(away, near_copy(s, k, 1 - d))
-                    src = chunk(near.at[d, s], k)
-                    start(away, near_copy(s, k, d, 2 if d else -2, src))
+                    mine = relayed_to(d)
+                    arrive(mine, near_copy(s, k, d))
+                    ship_piece(mine, 2 - d, s, k)
+
+    def take_far(s):
+        for d in range(2):
+            arrive(has_far[1 - d], far_copy(s, d))
+        for part in range(2):
+            wide[s, part] = unpack(far_in[0, s, part], far_in[1, s, part])
+        for part in range(2):
+            for d in range(2):
+                ship_tall(has_row[d], 3, s, part, d)
+
+    def take_places():
+        for d in range(2):
+            for moved in place_copies(d):
+                mine = has_col[1 - d]
+                arrive(both(mine, jnp.logical_not(relayed_to(d))) if detour else mine, moved)
+        if detour:
+            for d in range(2):
+                for moved in place_copies(1 - d, -2 if d else 2):
+                    start(outer(d), moved)
+            for d in range(2):
+                for moved in place_copies(d):
+                    arrive(relayed_to(d), moved)
 
     def hand_samples():
         if detour:
@@ -259,16 +310,6 @@
         for d in range(2):
             when = here(has_col[d], d)
             start(when if mine is None else both(when, mine), samples_copy(d))
-
-    for d in range(2):
-        start(has_col[d], corners_copy(d))
-        start(has_col[d], count_copy(d))
-    for s in slices:
-        if s < 2:
-            ship_near(s)
-        for d in range(2):
-            start(has_row[d], tall_copy(0, s, d))
-        ship_far(s)
 
     def clear(when, *refs):
         @pl.when(jnp.logical_not(when))
@@ -318,39 +359,35 @@
         found.live = j < (count[0, 0] if k == 1 else near_count[k // 2, 0, 0])
         return found
 
-    for d in range(2):
-        arrive(has_col[1 - d], corners_copy(d))
-        arrive(has_col[1 - d], count_copy(d))
+    loads[0].wait()
+    for s in slices:
+        for part in range(2):
+            for d, piece in enumerate(pack(field[s, part])):
+                far_out[d, s, part] = piece
+    pl.semaphore_wait(barrier, sum(there.astype(jnp.int32) for _, _, there in meets))
+    for s in slices:
+        if s < 2:
+            ship_near(s)
+        ship_far(s)
+        for part in range(2):
+            for d in range(2):
+                ship_tall(has_row[d], 0, s, part, d)
+        if s == 0:
+            for d in range(2):
+                for moved in place_copies(d):
+                    start(here(has_col[d], d), moved)
+    for load in loads[1:]:
+        load.wait()
     own_windows = [window_of(1, j) for j in range(slots)]
-    side_windows = [window_of(k, j) for k in (0, 2) for j in range(slots)]
-    load.wait()
-
-    def relay_on(s):
-        hand_lent(s)
-        hand_near(s)
-
-    def ship_tall(s):
-        for d in range(2):
-            for k in range(3):
-                mine = has_col[1 - d]
-                if detour and k < 2:
-                    mine = both(mine, jnp.logical_not(outer(d)))
-                arrive(mine, near_copy(s, k, d))
-        for d in range(2):
-            for e in range(2):
-                start(both(has_row[d], has_col[e]), tall_copy(1 + e, s, d))
-        for d in range(2):
-            arrive(has_far[1 - d], far_copy(s, d))
-        for part in range(2):
-            wide[s, part] = unpack(far_in[0, s, part], far_in[1, s, part])
-        for d in range(2):
-            start(has_row[d], tall_copy(3, s, d))
 
     def land_tall(s):
         for i in range(4):
-            for d in range(2):
-                there = has_row[1 - d] if i in (0, 3) else both(has_row[1 - d], has_col[i - 1])
-                arrive(there, tall_copy(i, s, d))
+            for part in range(2):
+                for d in range(2):
+                    there = has_row[1 - d]
+                    if i in (1, 2):
+                        there = both(there, has_col[i - 1])
+                    arrive(there, tall_copy(i, s, part, d))
 
     def spread(tiles, beyond, k):
         if k == 1:
@@ -435,24 +472,32 @@
         pieces = [[later[a, b, s, part] for part in range(2)] for a in range(2) for b in range(2)]
         return [cut(w, *pieces) for w in windows]
 
-    windows = own_windows + side_windows
-    waves = [w.beam for w in windows]
-    incident, layers = [], []
-    relay_on(0)
+    take_direct(0)
+    take_far(0)
+    hand_lent(0)
     for s in range(2, layer_count):
         ship_near(s)
     ends = jnp.logical_or(outer(0), outer(1))
     ship_samples(jnp.logical_not(ends) if detour else None)
-    ship_tall(0)
+    take_places()
+    side_windows = [window_of(k, j) for k in (0, 2) for j in range(slots)]
+    windows = own_windows + side_windows
+    waves = [w.beam for w in windows]
+    incident, layers = [], []
     for s in range(1, layer_count):
+        if s == 1:
+            take_direct(s)
+        take_far(s)
         hand_lent(s)
     if detour:
         ship_samples(ends)
+    take_relayed(0)
     for s in slices:
+        if s + 2 < layer_count:
+            take_direct(s + 2)
         if s + 1 < layer_count:
-            hand_near(s + 1)
-            ship_tall(s + 1)
-        else:
+            take_relayed(s + 1)
+        if s + 2 == layer_count:
             hand_samples()
         land_tall(s)
         incident.append(waves)
@@ -560,6 +605,7 @@
     tables = make_tables(probe.shape[-1])
     vmem = pl.BlockSpec(memory_space=pltpu.VMEM)
     smem = pl.BlockSpec(memory_space=pltpu.SMEM)
+    hbm = pl.BlockSpec(memory_space=pltpu.HBM)
     layer_count, _, side, _ = object_field.shape
     tiles = (layer_count, 2, side, side)
     packed = (2, layer_count, 2, side // 2, side)
@@ -585,9 +631,12 @@
     return pl.pallas_call(
         functools.partial(step_kernel, shape),
         out_shape=jax.ShapeDtypeStruct(object_field.shape, jnp.float32),
-        in_specs=[vmem, vmem, vmem, smem, smem, pl.BlockSpec(memory_space=pltpu.HBM)],
+        in_specs=[hbm, hbm, hbm, smem, smem, hbm],
         out_specs=vmem,
         scratch_shapes=[
+            pltpu.VMEM(tiles, jnp.float32),
+            pltpu.VMEM(probe.shape, jnp.float32),
+            pltpu.VMEM(samples.shape, jnp.float32),
             pltpu.VMEM(tables.shape, jnp.bfloat16),
             pltpu.VMEM((2,) + tiles, jnp.float32),
             pltpu.VMEM((2,) + samples.shape, jnp.float32),
@@ -598,7 +647,7 @@
         + [
             pltpu.SemaphoreType.DMA((COPIES,)),
             pltpu.SemaphoreType.DMA((COPIES,)),
-            pltpu.SemaphoreType.DMA,
+            pltpu.SemaphoreType.DMA((4,)),
         ],
         compiler_params=pltpu.CompilerParams(collective_id=0, has_side_effects=True),
         name="steps",

time: 56.9 us -> 56.4 us (level)
  the two profiles are of different devices: /device:TPU:18 before, /device:TPU:21 now
where the time goes in v2:
time: 56.4 us; the launch traced here: 56.2 us
  Pallas kernels  53.8 us (95%)
  local copies, waits for them, and re-layouts  1.77 us (3%)
  between operations  0.66 us (1%)
    pallas_call x1, Pallas kernels, shards(): pl.pallas_call(functools.partial(step_kernel, shape), out_shape=jax.Shape...  53.8 us
    unnamed x1, local copies, waits for them, and re-layouts  1.77 us

profile of v2, /device:TPU:21, one launch (start us, length us, event | category | flops | bytes accessed | tf_op | source)
XLA Modules:
  0.0 56.2 jit_solution(5870209643306434298)
XLA Ops:
  0.7 53.8 %steps.1 = f32[3,2,128,128]{3,2,1,0:T(8,128)} custom-call(f32[3,2,128,128]{3,2,1,0:T(8,128)} %field_far.1, f32[2,128,128]{2,1,0:T(8,128)} %probe_far.1, f32[2,128,128]{2,1,0:T(8,128)} %bitcast.1, s32[1,1,2,2]{3,2,1,0:T(2,128)} %corners.1, s32[1,1]{1,0:T(1,128)S(6)} %copy.8.count, bf16[4,2,256,256]{3,2,1,0:T(8,128)(2,1)} %constant.2.clone.table_far), custom_call_target="tpu_custom_call" | custom-call | tf_op jit(solution)/shard_map/steps/pallas_call | solution.py:631
  54.4 1.8 %copy.9 = f32[3,2,128,128]{3,2,1,0:T(8,128)} copy(f32[3,2,128,128]{3,2,1,0:T(8,128)} %steps.1) | data formatting | bytes 786432

commit v3 on v2

--- a/solution.py
+++ b/solution.py
@@ -41,6 +41,13 @@
 
 
 def both_sides(waves, table, form):
+    found = []
+    for at in range(0, len(waves), 2):
+        found += sides_of(waves[at : at + 2], table, form)
+    return found
+
+
+def sides_of(waves, table, form):
     side = waves[0][0].shape[0]
     stacked = jnp.concatenate([jnp.concatenate(pair, axis=1) for pair in waves], axis=0)
     lead, trail = split(stacked)
@@ -630,7 +637,7 @@
     ]
     return pl.pallas_call(
         functools.partial(step_kernel, shape),
-        out_shape=jax.ShapeDtypeStruct(object_field.shape, jnp.float32),
+        out_shape=pltpu.VMEM(object_field.shape, jnp.float32),
         in_specs=[hbm, hbm, hbm, smem, smem, hbm],
         out_specs=vmem,
         scratch_shapes=[

time: 56.4 us -> 53.1 us (0.941)
  the two profiles are of different devices: /device:TPU:21 before, /device:TPU:19 now
where the time goes in v3:
time: 53.1 us; the launch traced here: 52.9 us
  Pallas kernels  51.5 us (97%)
  local copies, waits for them, and re-layouts  0.75 us (1%)
  between operations  0.66 us (1%)
    pallas_call x1, Pallas kernels, shards(): pl.pallas_call(functools.partial(step_kernel, shape), out_shape=pltpu.VME...  51.5 us

profile of v3, /device:TPU:19, one launch (start us, length us, event | category | flops | bytes accessed | tf_op | source)
XLA Modules:
  0.0 52.9 jit_solution(8042154480713747104)
XLA Ops:
  0.7 51.5 %steps.1 = f32[3,2,128,128]{3,2,1,0:T(8,128)S(1)} custom-call(f32[3,2,128,128]{3,2,1,0:T(8,128)} %field_far.1, f32[2,128,128]{2,1,0:T(8,128)} %probe_far.1, f32[2,128,128]{2,1,0:T(8,128)} %bitcast.1, s32[1,1,2,2]{3,2,1,0:T(2,128)} %corners.1, s32[1,1]{1,0:T(1,128)S(6)} %copy.9.count, bf16[4,2,256,256]{3,2,1,0:T(8,128)(2,1)} %constant.2.clone.table_far), custom_call_target="tpu_custom_call" | custom-call | tf_op jit(solution)/shard_map/steps/pallas_call | solution.py:638
  52.1 0.7 %copy.8 = f32[3,2,128,128]{3,2,1,0:T(8,128)} copy(f32[3,2,128,128]{3,2,1,0:T(8,128)S(1)} %steps.1) | data formatting | bytes 786432

commit v4 on v3

--- a/solution.py
+++ b/solution.py
@@ -103,7 +103,7 @@
 def step_kernel(
     shape, field_far, probe_far, samples_far, corners, count, table_far, out,
     field, probe, samples, table, near, near_samples, near_corners, near_count, far_out, far_in, wide, tall,
-    grads, grads_in, later, kept, grad_rows, grad_in, grad_cols, fold_in, relay,
+    grads, grads_in, later, kept, grad_rows, grad_in, grad_cols, fold_in, cross_out, cross_in, summed, relay,
     send_sem, recv_sem, load_sem,
 ):
     layer_count = field.shape[0]
@@ -153,12 +153,29 @@
             device_id_type=pl.DeviceIdType.MESH,
         )
 
-    def start(when, moved):
-        pl.when(when)(moved.start)
-        started.append((when, moved))
-
-    def arrive(when, moved):
-        pl.when(when)(moved.wait_recv)
+    def start(when, *moves):
+        started.append((when, moves))
+
+        @pl.when(when)
+        def go():
+            for moved in moves:
+                moved.start()
+
+    def arrive(when, *moves):
+        @pl.when(when)
+        def stay():
+            for moved in moves:
+                moved.wait_recv()
+
+    def leave(count):
+        for when, moves in started[:count]:
+
+            @pl.when(when)
+            def gone():
+                for moved in moves:
+                    moved.wait_send()
+
+        del started[:count]
 
     def chunk(ref, k):
         return ref.at[0] if k == 0 else ref.at[1, parts[k - 1]]
@@ -204,18 +221,24 @@
 
     def fold_rows_copy(s, b, d):
         rows = parts[1 - d]
-        src, dst = grad_rows.at[s, b, :, rows], grad_in.at[s, b, :, rows]
+        src = grad_rows.at[s, b, :, rows]
+        if s == layer_count - 1:
+            src = summed.at[:, rows]
+        dst = grad_in.at[s, b, :, rows]
         return copy(("fold_rows", s, b, d), src, dst, "row", 1 if d else -1)
 
-    def fold_cols_copy(s, part, d, leg=0):
-        key = ("fold_cols", s, part, d)
-        src, dst = grad_cols.at[1 - d, s, part], fold_in.at[1 - d, s, part]
+    def fold_cols_copy(s, part, d, leg=0, cross=False):
+        key = ("cross" if cross else "fold_cols", s, part, d)
+        if cross:
+            src, dst, held = cross_out.at[1 - d, part], cross_in.at[1 - d, part], relay.at[2, s]
+        else:
+            src, dst = grad_cols.at[1 - d, s, part], fold_in.at[1 - d, s, part]
+            held = relay.at[1, s]
         step = 1 if d else -1
         if leg == 0:
             return copy(key, src, dst, "col", step)
-        held = relay.at[1, s]
         if leg == 1:
-            return copy(("lend_cols", s), src, held, "col", 2 * step)
+            return copy(("lend_" + key[0], s), src, held, "col", 2 * step)
         return copy(key, held, dst, "col", -step)
 
     barrier = pltpu.get_barrier_semaphore()
@@ -234,9 +257,8 @@
             )
 
     def ship_near(s):
-        for k in range(3):
-            for d in range(2):
-                start(here(has_col[d], d), near_copy(s, k, d))
+        for d in range(2):
+            start(here(has_col[d], d), *[near_copy(s, k, d) for k in range(3)])
 
     def ship_far(s):
         for d in range(2):
@@ -254,15 +276,16 @@
     def relayed_to(d):
         return (col == 1 + d) if detour else None
 
-    def ship_tall(when, i, s, part, d):
-        start(both(when, has_row[d]), tall_copy(i, s, part, d))
-
-    def ship_piece(when, i, s, k):
+    def piece_talls(i, s, k, d):
         if k == 0:
-            for d in range(2):
-                ship_tall(when, i, s, 0, d)
-        else:
-            ship_tall(when, i, s, 1, k - 1)
+            return [tall_copy(i, s, 0, d)]
+        return [tall_copy(i, s, 1, d)] if k - 1 == d else []
+
+    def ship_piece(mine, i, s, k):
+        for d in range(2):
+            moves = piece_talls(i, s, k, d)
+            if moves:
+                start(both(mine, has_row[d]), *moves)
 
     def take_direct(s):
         for k in range(3):
@@ -289,22 +312,20 @@
             arrive(has_far[1 - d], far_copy(s, d))
         for part in range(2):
             wide[s, part] = unpack(far_in[0, s, part], far_in[1, s, part])
-        for part in range(2):
-            for d in range(2):
-                ship_tall(has_row[d], 3, s, part, d)
+        for d in range(2):
+            start(has_row[d], *[tall_copy(3, s, part, d) for part in range(2)])
 
     def take_places():
         for d in range(2):
-            for moved in place_copies(d):
-                mine = has_col[1 - d]
-                arrive(both(mine, jnp.logical_not(relayed_to(d))) if detour else mine, moved)
+            mine = has_col[1 - d]
+            if detour:
+                mine = both(mine, jnp.logical_not(relayed_to(d)))
+            arrive(mine, *place_copies(d))
         if detour:
             for d in range(2):
-                for moved in place_copies(1 - d, -2 if d else 2):
-                    start(outer(d), moved)
-            for d in range(2):
-                for moved in place_copies(d):
-                    arrive(relayed_to(d), moved)
+                start(outer(d), *place_copies(1 - d, -2 if d else 2))
+            for d in range(2):
+                arrive(relayed_to(d), *place_copies(d))
 
     def hand_samples():
         if detour:
@@ -325,7 +346,8 @@
                 ref[...] = jnp.zeros(ref.shape, ref.dtype)
 
     for d in range(2):
-        clear(has_col[d], near.at[d], near_samples.at[d], tall.at[1 + d], fold_in.at[d])
+        clear(has_col[d], near.at[d], near_samples.at[d], tall.at[1 + d])
+        clear(has_col[d], fold_in.at[d], cross_in.at[d])
         clear(has_far[1 - d], far_in.at[d])
         rows = parts[1 - d]
         for s in slices:
@@ -376,25 +398,22 @@
         if s < 2:
             ship_near(s)
         ship_far(s)
-        for part in range(2):
-            for d in range(2):
-                ship_tall(has_row[d], 0, s, part, d)
+        for d in range(2):
+            start(has_row[d], *[tall_copy(0, s, part, d) for part in range(2)])
         if s == 0:
             for d in range(2):
-                for moved in place_copies(d):
-                    start(here(has_col[d], d), moved)
+                start(here(has_col[d], d), *place_copies(d))
     for load in loads[1:]:
         load.wait()
     own_windows = [window_of(1, j) for j in range(slots)]
 
     def land_tall(s):
-        for i in range(4):
-            for part in range(2):
-                for d in range(2):
-                    there = has_row[1 - d]
-                    if i in (1, 2):
-                        there = both(there, has_col[i - 1])
-                    arrive(there, tall_copy(i, s, part, d))
+        for d in range(2):
+            there = has_row[1 - d]
+            arrive(there, *[tall_copy(i, s, part, d) for i in (0, 3) for part in range(2)])
+            for i in (1, 2):
+                there = both(has_row[1 - d], has_col[i - 1])
+                arrive(there, *[tall_copy(i, s, part, d) for part in range(2)])
 
     def spread(tiles, beyond, k):
         if k == 1:
@@ -455,9 +474,8 @@
             start(has_row[d], grads_copy(s, a, d))
 
     def renew(s):
-        for a in range(2):
-            for d in range(2):
-                arrive(has_row[1 - d], grads_copy(s, a, d))
+        for d in range(2):
+            arrive(has_row[1 - d], *[grads_copy(s, a, d) for a in range(2)])
         top = lax.broadcasted_iota(jnp.int32, (side, side), 0) < half
         in_cols = jnp.where(first, has_col[1].astype(jnp.int32), has_col[0].astype(jnp.int32)) > 0
         in_rows = jnp.where(top, has_row[1].astype(jnp.int32), has_row[0].astype(jnp.int32)) > 0
@@ -517,6 +535,7 @@
         mine = has_col[1 - d]
         arrive(both(mine, jnp.logical_not(outer(d))) if detour else mine, samples_copy(d))
     back = both_sides(residues(far, windows), table, 1)
+    early = len(started)
     for s in reversed(slices):
         pieces = [conj_times(a, b) for a, b in zip(incident[s], back, strict=True)]
         gather_first(s, windows, pieces)
@@ -526,6 +545,8 @@
             back = both_sides(moved, table, 3)
     for s in slices:
         send_grads(s, 1)
+    leave(early)
+    early = len(started)
 
     windows = own_windows
     waves = [w.beam for w in windows]
@@ -552,58 +573,82 @@
             for b in range(2):
                 kept[b, s, part] = totals[0][b]
                 grad_rows[s, b, part] = totals[1][b]
-        for d in range(2):
-            start(has_row[d], fold_rows_copy(s, 1, d))
-
-    def ship_cols(s):
-        for d in range(2):
-            arrive(has_row[1 - d], fold_rows_copy(s, 1, d))
-        for part in range(2):
-            aside = kept[1, s, part] + grad_in[s, 1, part]
+
+    def send_cols(s, cross):
+        for part in (1, 0):
+            for d in range(2):
+                when = here(has_col[d], d) if part else has_col[d]
+                start(when, fold_cols_copy(s, part, d, 0, cross))
+                if detour and part:
+                    start(passed_on(d), fold_cols_copy(s, part, d, 1, cross))
+
+    def ship_cols(s, folded):
+        if folded:
+            for d in range(2):
+                arrive(has_row[1 - d], fold_rows_copy(s, 1, d))
+        for part in range(2):
+            aside = kept[1, s, part] + grad_in[s, 1, part] if folded else kept[1, s, part]
             for d, piece in enumerate(pack(aside)):
                 grad_cols[d, s, part] = piece
-        for part in (1, 0):
-            for d in range(2):
-                when = here(has_col[d], d) if part else has_col[d]
-                start(when, fold_cols_copy(s, part, d))
-                if detour and part:
-                    start(passed_on(d), fold_cols_copy(s, part, d, 1))
-
-    def hand_cols(s):
+        send_cols(s, False)
+
+    def ship_cross(s):
+        for part in range(2):
+            for d, piece in enumerate(pack(grad_rows[s, 1, part])):
+                cross_out[d, part] = piece
+        send_cols(s, True)
+
+    def hand_cols(s, cross=False):
         if detour:
             for d in range(2):
-                arrive(outer(d), fold_cols_copy(s, 1, d, 1))
-                start(outer(d), fold_cols_copy(s, 1, d, 2))
+                arrive(outer(d), fold_cols_copy(s, 1, d, 1, cross))
+                start(outer(d), fold_cols_copy(s, 1, d, 2, cross))
+
+    def send_rows(s, b):
+        for d in range(2):
+            start(has_row[d], fold_rows_copy(s, b, d))
+
+    def settle(s):
+        for d in range(2):
+            arrive(has_col[1 - d], *[fold_cols_copy(s, part, d, 0, True) for part in range(2)])
+        for part in range(2):
+            summed[part] = grad_rows[s, 0, part] + unpack(cross_in[0, part], cross_in[1, part])
+        send_rows(s, 0)
 
     def finish(s):
         for d in range(2):
             arrive(has_row[1 - d], fold_rows_copy(s, 0, d))
-            for part in range(2):
-                arrive(has_col[1 - d], fold_cols_copy(s, part, d))
+            arrive(has_col[1 - d], *[fold_cols_copy(s, part, d) for part in range(2)])
         for part in range(2):
             inner = kept[0, s, part] + grad_in[s, 0, part]
             total = inner + unpack(fold_in[0, s, part], fold_in[1, s, part])
             out[s, part] = later[0, 0, s, part] - LEARNING_RATE * total
 
+    last = layer_count - 1
     for s in reversed(slices):
         gather_second(s, [conj_times(a, b) for a, b in zip(incident[s], back, strict=True)])
-        if s + 1 < layer_count:
-            ship_cols(s + 1)
+        if s == last:
+            ship_cross(s)
+            ship_cols(s, False)
+        else:
+            send_rows(s, 1)
         if s > 0:
             moved = [conj_times(a, b) for a, b in zip(layers[s], back, strict=True)]
             back = both_sides(moved, table, 3)
-    for s in reversed(slices):
-        for d in range(2):
-            start(has_row[d], fold_rows_copy(s, 0, d))
-    for s in range(layer_count - 1, 1, -1):
+    for s in reversed(range(last)):
+        send_rows(s, 0)
+    hand_cols(last, True)
+    hand_cols(last)
+    for s in reversed(range(last)):
+        ship_cols(s, True)
+    leave(early)
+    settle(last)
+    for s in reversed(range(last)):
         hand_cols(s)
-    ship_cols(0)
-    for s in reversed(range(min(2, layer_count))):
-        hand_cols(s)
-    for s in reversed(slices):
+    for s in reversed(slices[:last]):
         finish(s)
-    for when, moved in started:
-        pl.when(when)(moved.wait_send)
+    finish(last)
+    leave(len(started))
     assert len(numbers) <= COPIES
 
 
@@ -632,7 +677,10 @@
             (layer_count, 2, 2, side, side),
             packed,
             packed,
-            (2, layer_count, side // 2, side),
+            packed[:1] + packed[2:],
+            packed[:1] + packed[2:],
+            tiles[1:],
+            (3, layer_count, side // 2, side),
         )
     ]
     return pl.pallas_call(

time: 53.1 us -> 51.7 us (0.974)
  the two profiles are of different devices: /device:TPU:19 before, /device:TPU:18 now
where the time goes in v4:
time: 51.7 us; the launch traced here: 50.8 us
  Pallas kernels  49.4 us (96%)
  local copies, waits for them, and re-layouts  0.75 us (1%)
  between operations  0.66 us (1%)
    pallas_call x1, Pallas kernels, shards(): pl.pallas_call(functools.partial(step_kernel, shape), out_shape=pltpu.VME...  49.4 us

profile of v4, /device:TPU:18, one launch (start us, length us, event | category | flops | bytes accessed | tf_op | source)
XLA Modules:
  0.0 50.8 jit_solution(135435940438373760)
XLA Ops:
  0.7 49.4 %steps.1 = f32[3,2,128,128]{3,2,1,0:T(8,128)S(1)} custom-call(f32[3,2,128,128]{3,2,1,0:T(8,128)} %field_far.1, f32[2,128,128]{2,1,0:T(8,128)} %probe_far.1, f32[2,128,128]{2,1,0:T(8,128)} %bitcast.1, s32[1,1,2,2]{3,2,1,0:T(2,128)} %corners.1, s32[1,1]{1,0:T(1,128)S(6)} %copy.9.count, bf16[4,2,256,256]{3,2,1,0:T(8,128)(2,1)} %constant.2.clone.table_far), custom_call_target="tpu_custom_call" | custom-call | tf_op jit(solution)/shard_map/steps/pallas_call | solution.py:686
  50.0 0.7 %copy.8 = f32[3,2,128,128]{3,2,1,0:T(8,128)} copy(f32[3,2,128,128]{3,2,1,0:T(8,128)S(1)} %steps.1) | data formatting | bytes 786432

commit v5 on v4

--- a/solution.py
+++ b/solution.py
@@ -575,12 +575,13 @@
                 grad_rows[s, b, part] = totals[1][b]
 
     def send_cols(s, cross):
-        for part in (1, 0):
-            for d in range(2):
-                when = here(has_col[d], d) if part else has_col[d]
-                start(when, fold_cols_copy(s, part, d, 0, cross))
-                if detour and part:
-                    start(passed_on(d), fold_cols_copy(s, part, d, 1, cross))
+        if detour:
+            for d in range(2):
+                lent, direct = [fold_cols_copy(s, leg, d, leg, cross) for leg in (1, 0)]
+                start(passed_on(d), lent, direct)
+        for d in range(2):
+            moves = [fold_cols_copy(s, part, d, 0, cross) for part in (1, 0)]
+            start(here(has_col[d], d), *moves)
 
     def ship_cols(s, folded):
         if folded:

time: 51.7 us -> 52.5 us (1.015)
  the two profiles are of different devices: /device:TPU:18 before, /device:TPU:0 now
where the time goes in v5:
time: 52.5 us; the launch traced here: 52.3 us
  Pallas kernels  50.9 us (97%)
  local copies, waits for them, and re-layouts  0.75 us (1%)
  between operations  0.66 us (1%)
    pallas_call x1, Pallas kernels, shards(): pl.pallas_call(functools.partial(step_kernel, shape), out_shape=pltpu.VME...  50.9 us

profile of v5, /device:TPU:0, one launch (start us, length us, event | category | flops | bytes accessed | tf_op | source)
XLA Modules:
  0.0 52.3 jit_solution(2183195640768867948)
XLA Ops:
  0.7 50.9 %steps.1 = f32[3,2,128,128]{3,2,1,0:T(8,128)S(1)} custom-call(f32[3,2,128,128]{3,2,1,0:T(8,128)} %field_far.1, f32[2,128,128]{2,1,0:T(8,128)} %probe_far.1, f32[2,128,128]{2,1,0:T(8,128)} %bitcast.1, s32[1,1,2,2]{3,2,1,0:T(2,128)} %corners.1, s32[1,1]{1,0:T(1,128)S(6)} %copy.9.count, bf16[4,2,256,256]{3,2,1,0:T(8,128)(2,1)} %constant.2.clone.table_far), custom_call_target="tpu_custom_call" | custom-call | tf_op jit(solution)/shard_map/steps/pallas_call | solution.py:687
  51.6 0.7 %copy.8 = f32[3,2,128,128]{3,2,1,0:T(8,128)} copy(f32[3,2,128,128]{3,2,1,0:T(8,128)S(1)} %steps.1) | data formatting | bytes 786432
